TPU v7x, 32 devices: a whole 2x2x4 slice. The times are simulated.
32 devices in a mesh: row: 4 (over y, x), col: 8 (over z, core).
Axes of the slice: x: 2, y: 2, z: 4, core: 2. Of those that a mesh axis runs over, the one named last changes fastest.
Arguments:
- left_matrix: float32 [4096, 4096], P('row', 'col'), may hold values from -6 to 6
- right_matrix: float32 [4096, 4096], P('row', 'col'), may hold values from -0.09375 to 0.09375
Outputs:
- product_matrix: float32 [4096, 4096], P('row', 'col')
All inputs are finite; a program needn't handle non-finite values.
Results may differ from a plain program's by a relative error of at most 0.00019.
Values sent between devices are 32-bit elements; how exact they have to be, the bound alone decides.
A program may use at most 64 MiB of HBM per device.

v0:
```python
import jax
import jax.numpy as jnp
from jax import lax
from jax.sharding import PartitionSpec as P


def multiply(left_term, right_term):
    return jnp.dot(
        left_term, right_term, precision=lax.Precision.HIGHEST, preferred_element_type=jnp.float32
    )


def body(left_matrix, right_matrix):
    row_panel = lax.all_gather(left_matrix, "col", axis=1, tiled=True)
    col_panel = lax.all_gather(right_matrix, "row", axis=0, tiled=True)
    return multiply(row_panel, col_panel)


def solution(mesh):
    placed = (P("row", "col"), P("row", "col"))
    return jax.shard_map(
        body, mesh=mesh, in_specs=placed, out_specs=P("row", "col"), check_vma=False
    )
```

profile of v0, /device:TPU:0, one launch (start us, length us, event | category | flops | bytes accessed | tf_op | source)
XLA Modules:
  0.0 289.9 jit_solution(7672909341723281923)
XLA Ops:
  6.5 0.0 all-gather.5.cloned.1.call-start
  6.5 0.7 all-gather.5.cloned.1.call-update
  7.3 0.0 all-gather.3.cloned.1.call-start
  7.3 0.7 all-gather.3.cloned.1.call-update
  8.0 91.4 %all-gather.5.cloned.1.call-done = f32[4096,512]{1,0:T(8,128)} async-done(((f32[1024,512]{1,0:T(8,128)}), f32[4096,512]{1,0:T(8,128)}) %all-gather.5.cloned.1.call-update) | async-done | bytes 8388624 | tf_op jit(solution)/shard_map/all_gather | solution.py:15
  99.4 152.7 %all-gather.3.cloned.1.call-done = f32[1024,4096]{1,0:T(8,128)} async-done(((f32[1024,512]{1,0:T(8,128)}), f32[1024,4096]{1,0:T(8,128)}) %all-gather.3.cloned.1.call-update) | async-done | bytes 16777232 | tf_op jit(solution)/shard_map/all_gather | solution.py:14
  252.1 31.0 %fusion = f32[1024,512]{1,0:T(8,128)} fusion(f32[1024,4096]{1,0:T(8,128)} %all-gather.3.cloned.1.call-done, f32[4096,512]{1,0:T(8,128)} %all-gather.5.cloned.1.call-done), kind=kOutput, calls=%fused_computation | convolution fusion | flops 25769803776 | bytes 27262976 | tf_op jit(solution)/shard_map/dot_general | solution.py:8
Async XLA Ops:
  6.5 92.9 %all-gather.5.cloned.1.call-start = ((), (), s32[]{:S(2)}) async-start(), calls=%async_computation.1 | async-start | bytes 10485760 | tf_op jit(solution)/shard_map/all_gather | solution.py:15
  7.3 244.9 %all-gather.3.cloned.1.call-start = ((), (), s32[]{:S(2)}) async-start(), calls=%async_computation | async-start | bytes 18874368 | tf_op jit(solution)/shard_map/all_gather | solution.py:14
Sparse Core Ops, SparseCore 0:
  9.2 90.1 all-gather.4
  101.0 151.0 all-gather.2
where the time goes:
time: 290 us
  waiting for transfers between devices  246 us (85%)
  matrix products  31 us (11%)
  between operations  13.4 us (5%)
    all_gather x1, waiting for transfers between devices, body(): row_panel = lax.all_gather(left_matrix, 'col', axis=1, tiled=True)  153 us
    all_gather x1, waiting for transfers between devices, body(): col_panel = lax.all_gather(right_matrix, 'row', axis=0, tiled=True)  91.4 us
    dot_general x1, matrix products, multiply(): jnp.dot(left_term, right_term, precision=lax.Precision.HIGHEST, preferred...  31 us
  transfers between devices with their start and end apart: 2, of which 2 were waited for; matrix products, arithmetic and copies ran while one was open for 0% of the time, Pallas kernels for 0%

commit v1 on v0

--- a/solution.py
+++ b/solution.py
@@ -11,7 +11,12 @@
 
 
 def body(left_matrix, right_matrix):
-    row_panel = lax.all_gather(left_matrix, "col", axis=1, tiled=True)
+    ring = [left_matrix]
+    for hop in range(7):
+        ring.append(lax.ppermute(ring[-1], "col", [(dev, (dev + 1) % 8) for dev in range(8)]))
+    row_panel = jnp.roll(
+        jnp.concatenate(ring[::-1], axis=1), (lax.axis_index("col") + 1) * ring[0].shape[1], axis=1
+    )
     col_panel = lax.all_gather(right_matrix, "row", axis=0, tiled=True)
     return multiply(row_panel, col_panel)
 

time: 290 us -> 285 us (0.983)
  waiting for transfers between devices: 246 us -> 193 us
  local copies, waits for them, and re-layouts: 0 us -> 46.6 us
    ppermute x0 -> x7, waiting for transfers between devices: none -> 193 us  [body(): lax.ppermute(ring[-1], 'col', [(dev, (dev + 1) % 8) for dev in range(8)])]
    all_gather x1 -> x0, waiting for transfers between devices: 153 us -> none  [body(): row_panel = lax.all_gather(left_matrix, 'col', axis=1, tiled=True)]
    all_gather x1, waiting for transfers between devices: 91.4 us -> 0.01 us  [body(): col_panel = lax.all_gather(right_matrix, 'row', axis=0, tiled=True)]
    unnamed x0 -> x29, local copies, waits for them, and re-layouts: none -> 45.1 us
  transfers between devices with their start and end apart: 2 -> 8, of which waited for: 2 -> 7; matrix products, arithmetic and copies ran while one was open for 0% -> 15% of each run, Pallas kernels for 0% -> 0%
where the time goes in v1:
time: 285 us; the launch traced here: 284 us
  waiting for transfers between devices  193 us (68%)
  local copies, waits for them, and re-layouts  46.6 us (16%)
  matrix products  31 us (11%)
  between operations  13.4 us (5%)
    ppermute x7, waiting for transfers between devices, body(): lax.ppermute(ring[-1], 'col', [(dev, (dev + 1) % 8) for dev in range(8)])  193 us
    unnamed x29, local copies, waits for them, and re-layouts  45.1 us
    dot_general x1, matrix products, multiply(): jnp.dot(left_term, right_term, precision=lax.Precision.HIGHEST, preferred...  31 us
  transfers between devices with their start and end apart: 8, of which 7 were waited for; matrix products, arithmetic and copies ran while one was open for 15% of the time, Pallas kernels for 0%

profile of v1, /device:TPU:0, one launch (start us, length us, event | category | flops | bytes accessed | tf_op | source)
XLA Modules:
  0.0 284.1 jit_solution(11674482978669563647)
XLA Ops:
  6.5 0.5 collective-permute-start
  7.0 28.0 %collective-permute-done = f32[1024,512]{1,0:T(8,128)S(1)} collective-permute-done((f32[1024,512]{1,0:T(8,128)}, f32[1024,512]{1,0:T(8,128)S(1)}, u32[]{:S(2)}, u32[]{:S(2)}) %collective-permute-start) | collective-permute-done | bytes 2097184 | tf_op jit(solution)/shard_map/ppermute | solution.py:16
  35.1 1.4 copy-done.1
  36.4 0.0 collective-permute-start.1
  36.4 27.4 %collective-permute-done.1 = f32[1024,512]{1,0:T(8,128)} collective-permute-done((f32[1024,512]{1,0:T(8,128)S(1)}, f32[1024,512]{1,0:T(8,128)}, u32[]{:S(2)}, u32[]{:S(2)}) %collective-permute-start.1) | collective-permute-done | bytes 2097184 | tf_op jit(solution)/shard_map/ppermute | solution.py:16
  63.8 0.0 collective-permute-start.2
  63.8 0.0 all-gather.2.cloned.1.call-update
  63.8 27.5 %collective-permute-done.2 = f32[1024,512]{1,0:T(8,128)} collective-permute-done((f32[1024,512]{1,0:T(8,128)}, f32[1024,512]{1,0:T(8,128)}, u32[]{:S(2)}, u32[]{:S(2)}) %collective-permute-start.2) | collective-permute-done | bytes 2097184 | tf_op jit(solution)/shard_map/ppermute | solution.py:16
  91.4 0.0 collective-permute-start.3
  91.4 27.5 %collective-permute-done.3 = f32[1024,512]{1,0:T(8,128)S(1)} collective-permute-done((f32[1024,512]{1,0:T(8,128)}, f32[1024,512]{1,0:T(8,128)S(1)}, u32[]{:S(2)}, u32[]{:S(2)}) %collective-permute-start.3) | collective-permute-done | bytes 2097184 | tf_op jit(solution)/shard_map/ppermute | solution.py:16
  118.8 1.3 copy-done.3
  120.2 27.3 %collective-permute-done.4 = f32[1024,512]{1,0:T(8,128)S(1)} collective-permute-done((f32[1024,512]{1,0:T(8,128)S(1)}, f32[1024,512]{1,0:T(8,128)S(1)}, u32[]{:S(2)}, u32[]{:S(2)}) %collective-permute-start.4) | collective-permute-done | bytes 2097184 | tf_op jit(solution)/shard_map/ppermute | solution.py:16
  147.4 1.3 copy-done.5
  148.7 27.4 %collective-permute-done.5 = f32[1024,512]{1,0:T(8,128)} collective-permute-done((f32[1024,512]{1,0:T(8,128)S(1)}, f32[1024,512]{1,0:T(8,128)}, u32[]{:S(2)}, u32[]{:S(2)}) %collective-permute-start.5) | collective-permute-done | bytes 2097184 | tf_op jit(solution)/shard_map/ppermute | solution.py:16
  176.1 27.6 %collective-permute-done.6 = f32[1024,512]{1,0:T(8,128)} collective-permute-done((f32[1024,512]{1,0:T(8,128)}, f32[1024,512]{1,0:T(8,128)}, u32[]{:S(2)}, u32[]{:S(2)}) %collective-permute-start.6) | collective-permute-done | bytes 2097184 | tf_op jit(solution)/shard_map/ppermute | solution.py:16
  203.7 3.1 %constant_dynamic-update-slice_fusion.15 = f32[1024,8192]{1,0:T(8,128)} fusion(f32[1024,512]{1,0:T(8,128)} %collective-permute-done.6), kind=kLoop, calls=%fused_computation.17 | loop fusion | bytes 4194304
  206.7 3.0 %constant_dynamic-update-slice_fusion.14 = f32[1024,8192]{1,0:T(8,128)} fusion(f32[1024,8192]{1,0:T(8,128)} %constant_dynamic-update-slice_fusion.15, f32[1024,512]{1,0:T(8,128)} %collective-permute-done.5), kind=kLoop, calls=%fused_computation.16 | loop fusion | bytes 4194304
  209.8 3.1 %constant_dynamic-update-slice_fusion.13 = f32[1024,8192]{1,0:T(8,128)} fusion(f32[1024,8192]{1,0:T(8,128)} %constant_dynamic-update-slice_fusion.14, f32[1024,512]{1,0:T(8,128)} %copy-done.5), kind=kLoop, calls=%fused_computation.15 | loop fusion | bytes 4194304
  212.8 3.0 %constant_dynamic-update-slice_fusion.12 = f32[1024,8192]{1,0:T(8,128)} fusion(f32[1024,8192]{1,0:T(8,128)} %constant_dynamic-update-slice_fusion.13, f32[1024,512]{1,0:T(8,128)} %copy-done.3), kind=kLoop, calls=%fused_computation.14 | loop fusion | bytes 4194304
  215.9 3.0 %constant_dynamic-update-slice_fusion.11 = f32[1024,8192]{1,0:T(8,128)} fusion(f32[1024,8192]{1,0:T(8,128)} %constant_dynamic-update-slice_fusion.12, f32[1024,512]{1,0:T(8,128)} %collective-permute-done.2), kind=kLoop, calls=%fused_computation.13 | loop fusion | bytes 4194304
  218.9 3.1 %constant_dynamic-update-slice_fusion.10 = f32[1024,8192]{1,0:T(8,128)} fusion(f32[1024,8192]{1,0:T(8,128)} %constant_dynamic-update-slice_fusion.11, f32[1024,512]{1,0:T(8,128)} %collective-permute-done.1), kind=kLoop, calls=%fused_computation.12 | loop fusion | bytes 4194304
  222.0 3.1 %constant_dynamic-update-slice_fusion.9 = f32[1024,8192]{1,0:T(8,128)} fusion(f32[1024,8192]{1,0:T(8,128)} %constant_dynamic-update-slice_fusion.10, f32[1024,512]{1,0:T(8,128)} %copy-done.1), kind=kLoop, calls=%fused_computation.11 | loop fusion | bytes 4194304
  225.0 3.1 %constant_dynamic-update-slice_fusion.8 = f32[1024,8192]{1,0:T(8,128)} fusion(f32[1024,8192]{1,0:T(8,128)} %constant_dynamic-update-slice_fusion.9, f32[1024,512]{1,0:T(8,128)} %param.2), kind=kLoop, calls=%fused_computation.10 | loop fusion | bytes 4194304
  228.1 3.1 %constant_dynamic-update-slice_fusion.7 = f32[1024,8192]{1,0:T(8,128)} fusion(f32[1024,8192]{1,0:T(8,128)} %constant_dynamic-update-slice_fusion.8, f32[1024,512]{1,0:T(8,128)} %collective-permute-done.6), kind=kLoop, calls=%fused_computation.9 | loop fusion | bytes 4194304
  231.2 3.1 %constant_dynamic-update-slice_fusion.6 = f32[1024,8192]{1,0:T(8,128)} fusion(f32[1024,8192]{1,0:T(8,128)} %constant_dynamic-update-slice_fusion.7, f32[1024,512]{1,0:T(8,128)} %collective-permute-done.5), kind=kLoop, calls=%fused_computation.8 | loop fusion | bytes 4194304
  234.2 1.5 constant_dynamic-update-slice_fusion.5
  235.7 1.5 constant_dynamic-update-slice_fusion.4
  237.2 3.1 %constant_dynamic-update-slice_fusion.3 = f32[1024,8192]{1,0:T(8,128)} fusion(f32[1024,8192]{1,0:T(8,128)} %constant_dynamic-update-slice_fusion.4, f32[1024,512]{1,0:T(8,128)} %collective-permute-done.2), kind=kLoop, calls=%fused_computation.5 | loop fusion | bytes 4194304
  240.2 3.1 %constant_dynamic-update-slice_fusion.2 = f32[1024,8192]{1,0:T(8,128)} fusion(f32[1024,8192]{1,0:T(8,128)} %constant_dynamic-update-slice_fusion.3, f32[1024,512]{1,0:T(8,128)} %collective-permute-done.1), kind=kLoop, calls=%fused_computation.4 | loop fusion | bytes 4194304
  243.3 1.5 constant_dynamic-update-slice_fusion.1
  244.8 1.5 constant_dynamic-update-slice_fusion
  246.3 31.0 %fusion = f32[1024,512]{1,0:T(8,128)} fusion(f32[4096,512]{1,0:T(8,128)} %all-gather.2.cloned.1.call-done, f32[1024,8192]{1,0:T(8,128)} %constant_dynamic-update-slice_fusion, s32[]{:T(128)S(6)} %select_n.14), kind=kOutput, calls=%fused_computation | convolution fusion | flops 25769803776 | bytes 27262980 | tf_op jit(solution)/shard_map/dot_general | solution.py:8
  (16 shorter events, 0.0 us)
Async XLA Ops:
  6.5 238.3 %copy-start = (f32[1024,512]{1,0:T(8,128)S(1)}, f32[1024,512]{1,0:T(8,128)}, u32[]{:S(2)}) copy-start(f32[1024,512]{1,0:T(8,128)} %param.2) | copy-start | bytes 6291460
  6.5 239.7 %all-gather.2.cloned.1.call-start = ((), (), s32[]{:S(2)}) async-start(), calls=%async_computation | async-start | bytes 10485760 | tf_op jit(solution)/shard_map/all_gather | solution.py:20
  6.5 28.5 %collective-permute-start = (f32[1024,512]{1,0:T(8,128)}, f32[1024,512]{1,0:T(8,128)S(1)}, u32[]{:S(2)}, u32[]{:S(2)}) collective-permute-start(f32[1024,512]{1,0:T(8,128)} %param.2), channel_id=1, source_target_pairs={{0,1},{1,2},{2,3},{3,4},{4,5},{5,6},{6,7},{7,0},{8,9},{9,10},{10,1... | collective-permute-start | bytes 6291464 | tf_op jit(solution)/shard_map/ppermute | solution.py:16
  35.1 1.4 copy-start.1
  36.4 27.4 %collective-permute-start.1 = (f32[1024,512]{1,0:T(8,128)S(1)}, f32[1024,512]{1,0:T(8,128)}, u32[]{:S(2)}, u32[]{:S(2)}) collective-permute-start(f32[1024,512]{1,0:T(8,128)S(1)} %collective-permute-done), channel_id=1, source_target_pairs={{0,1},{1,2},{2,3},{3,4},{4,5},{5,6},{6,7},{7,0},{8,9},{9,10},{10,1... | collective-permute-start | bytes 6291464 | tf_op jit(solution)/shard_map/ppermute | solution.py:16
  63.8 27.6 %collective-permute-start.2 = (f32[1024,512]{1,0:T(8,128)}, f32[1024,512]{1,0:T(8,128)}, u32[]{:S(2)}, u32[]{:S(2)}) collective-permute-start(f32[1024,512]{1,0:T(8,128)} %collective-permute-done.1), channel_id=1, source_target_pairs={{0,1},{1,2},{2,3},{3,4},{4,5},{5,6},{6,7},{7,0},{8,9},{9,10},{10,1... | collective-permute-start | bytes 6291464 | tf_op jit(solution)/shard_map/ppermute | solution.py:16
  91.4 27.5 %collective-permute-start.3 = (f32[1024,512]{1,0:T(8,128)}, f32[1024,512]{1,0:T(8,128)S(1)}, u32[]{:S(2)}, u32[]{:S(2)}) collective-permute-start(f32[1024,512]{1,0:T(8,128)} %collective-permute-done.2), channel_id=1, source_target_pairs={{0,1},{1,2},{2,3},{3,4},{4,5},{5,6},{6,7},{7,0},{8,9},{9,10},{10,1... | collective-permute-start | bytes 6291464 | tf_op jit(solution)/shard_map/ppermute | solution.py:16
  118.8 1.3 copy-start.3
  120.2 27.3 %collective-permute-start.4 = (f32[1024,512]{1,0:T(8,128)S(1)}, f32[1024,512]{1,0:T(8,128)S(1)}, u32[]{:S(2)}, u32[]{:S(2)}) collective-permute-start(f32[1024,512]{1,0:T(8,128)S(1)} %collective-permute-done.3), channel_id=1, source_target_pairs={{0,1},{1,2},{2,3},{3,4},{4,5},{5,6},{6,7},{7,0},{8,9},{9,10},{10,1... | collective-permute-start | bytes 6291464 | tf_op jit(solution)/shard_map/ppermute | solution.py:16
  147.4 1.3 copy-start.5
  148.7 27.4 %collective-permute-start.5 = (f32[1024,512]{1,0:T(8,128)S(1)}, f32[1024,512]{1,0:T(8,128)}, u32[]{:S(2)}, u32[]{:S(2)}) collective-permute-start(f32[1024,512]{1,0:T(8,128)S(1)} %collective-permute-done.4), channel_id=1, source_target_pairs={{0,1},{1,2},{2,3},{3,4},{4,5},{5,6},{6,7},{7,0},{8,9},{9,10},{10,1... | collective-permute-start | bytes 6291464 | tf_op jit(solution)/shard_map/ppermute | solution.py:16
  176.1 27.6 %collective-permute-start.6 = (f32[1024,512]{1,0:T(8,128)}, f32[1024,512]{1,0:T(8,128)}, u32[]{:S(2)}, u32[]{:S(2)}) collective-permute-start(f32[1024,512]{1,0:T(8,128)} %collective-permute-done.5), channel_id=1, source_target_pairs={{0,1},{1,2},{2,3},{3,4},{4,5},{5,6},{6,7},{7,0},{8,9},{9,10},{10,1... | collective-permute-start | bytes 6291464 | tf_op jit(solution)/shard_map/ppermute | solution.py:16
  176.1 58.1 %copy-start.6 = (f32[1024,512]{1,0:T(8,128)S(1)}, f32[1024,512]{1,0:T(8,128)}, u32[]{:S(2)}) copy-start(f32[1024,512]{1,0:T(8,128)} %copy-done.5) | copy-start | bytes 6291460
  176.1 59.6 %copy-start.4 = (f32[1024,512]{1,0:T(8,128)S(1)}, f32[1024,512]{1,0:T(8,128)}, u32[]{:S(2)}) copy-start(f32[1024,512]{1,0:T(8,128)} %copy-done.3) | copy-start | bytes 6291460
  176.1 67.2 %copy-start.2 = (f32[1024,512]{1,0:T(8,128)S(1)}, f32[1024,512]{1,0:T(8,128)}, u32[]{:S(2)}) copy-start(f32[1024,512]{1,0:T(8,128)} %copy-done.1) | copy-start | bytes 6291460
Sparse Core Ops, SparseCore 0:
  63.9 89.1 all-gather.1

commit v2 on v0

--- a/solution.py
+++ b/solution.py
@@ -12,7 +12,12 @@
 
 def body(left_matrix, right_matrix):
     row_panel = lax.all_gather(left_matrix, "col", axis=1, tiled=True)
-    col_panel = lax.all_gather(right_matrix, "row", axis=0, tiled=True)
+    ring = [right_matrix]
+    for hop in range(3):
+        ring.append(lax.ppermute(ring[-1], "row", [(dev, (dev + 1) % 4) for dev in range(4)]))
+    col_panel = jnp.roll(
+        jnp.concatenate(ring[::-1], axis=0), (lax.axis_index("row") + 1) * ring[0].shape[0], axis=0
+    )
     return multiply(row_panel, col_panel)
 
 

time: 290 us -> 240 us (0.83)
  waiting for transfers between devices: 246 us -> 142 us
  local copies, waits for them, and re-layouts: 0 us -> 24.7 us
  matrix products: 31 us -> 55.6 us
  starting transfers between devices: 0.04 us -> 3.81 us
    all_gather x1, waiting for transfers between devices: 153 us -> 0.01 us  [body(): row_panel = lax.all_gather(left_matrix, 'col', axis=1, tiled=True)]
    ppermute x0 -> x3, waiting for transfers between devices: none -> 141 us  [body(): lax.ppermute(ring[-1], 'row', [(dev, (dev + 1) % 4) for dev in range(4)])]
    all_gather x1 -> x0, waiting for transfers between devices: 91.4 us -> none  [body(): col_panel = lax.all_gather(right_matrix, 'row', axis=0, tiled=True)]
    dot_general x1, matrix products: 31 us -> 55.6 us  [multiply(): jnp.dot(left_term, right_term, precision=lax.Precision.HIGHEST, preferred...]
    unnamed x0 -> x13, local copies, waits for them, and re-layouts: none -> 21.5 us
    ppermute x0 -> x3, starting transfers between devices: none -> 3.8 us  [body(): lax.ppermute(ring[-1], 'row', [(dev, (dev + 1) % 4) for dev in range(4)])]
  transfers between devices with their start and end apart: 2 -> 4, of which waited for: 2 -> 3; matrix products, arithmetic and copies ran while one was open for 0% -> 9% of each run, Pallas kernels for 0% -> 0%
where the time goes in v2:
time: 240 us; the launch traced here: 239 us
  waiting for transfers between devices  142 us (59%)
  matrix products  55.6 us (23%)
  local copies, waits for them, and re-layouts  24.7 us (10%)
  between operations  13.4 us (6%)
  starting transfers between devices  3.81 us (2%)
    ppermute x3, waiting for transfers between devices, body(): lax.ppermute(ring[-1], 'row', [(dev, (dev + 1) % 4) for dev in range(4)])  141 us
    dot_general x1, matrix products, multiply(): jnp.dot(left_term, right_term, precision=lax.Precision.HIGHEST, preferred...  55.6 us
    unnamed x13, local copies, waits for them, and re-layouts  21.5 us
  transfers between devices with their start and end apart: 4, of which 3 were waited for; matrix products, arithmetic and copies ran while one was open for 9% of the time, Pallas kernels for 0%

profile of v2, /device:TPU:0, one launch (start us, length us, event | category | flops | bytes accessed | tf_op | source)
XLA Modules:
  0.0 239.4 jit_solution(10999509172959733152)
XLA Ops:
  6.5 0.0 copy-start
  6.5 0.0 all-gather.2.cloned.1.call-start
  6.5 0.7 all-gather.2.cloned.1.call-update
  7.3 3.0 %collective-permute-start = (f32[1024,512]{1,0:T(8,128)}, f32[1024,512]{1,0:T(8,128)S(1)}, u32[]{:S(2)}, u32[]{:S(2)}) collective-permute-start(f32[1024,512]{1,0:T(8,128)} %param.3), channel_id=1, source_target_pairs={{0,8},{8,16},{16,24},{24,0},{1,9},{9,17},{17,25},{25,1},{2,10},{10... | collective-permute-start | bytes 6291464 | tf_op jit(solution)/shard_map/ppermute | solution.py:17
  10.3 46.8 %collective-permute-done = f32[1024,512]{1,0:T(8,128)S(1)} collective-permute-done((f32[1024,512]{1,0:T(8,128)}, f32[1024,512]{1,0:T(8,128)S(1)}, u32[]{:S(2)}, u32[]{:S(2)}) %collective-permute-start) | collective-permute-done | bytes 2097184 | tf_op jit(solution)/shard_map/ppermute | solution.py:17
  57.1 0.0 copy-start.1
  57.1 1.3 copy-done.1
  58.4 0.8 collective-permute-start.1
  59.2 47.1 %collective-permute-done.1 = f32[1024,512]{1,0:T(8,128)} collective-permute-done((f32[1024,512]{1,0:T(8,128)S(1)}, f32[1024,512]{1,0:T(8,128)}, u32[]{:S(2)}, u32[]{:S(2)}) %collective-permute-start.1) | collective-permute-done | bytes 2097184 | tf_op jit(solution)/shard_map/ppermute | solution.py:17
  106.3 0.0 collective-permute-start.2
  106.3 0.0 copy-start.2
  106.3 47.3 %collective-permute-done.2 = f32[1024,512]{1,0:T(8,128)} collective-permute-done((f32[1024,512]{1,0:T(8,128)}, f32[1024,512]{1,0:T(8,128)}, u32[]{:S(2)}, u32[]{:S(2)}) %collective-permute-start.2) | collective-permute-done | bytes 2097184 | tf_op jit(solution)/shard_map/ppermute | solution.py:17
  153.6 3.2 %constant_dynamic-update-slice_fusion.7 = f32[8192,512]{1,0:T(8,128)} fusion(f32[1024,512]{1,0:T(8,128)} %collective-permute-done.2), kind=kLoop, calls=%fused_computation.10 | loop fusion | bytes 4194304
  156.7 3.1 %constant_dynamic-update-slice_fusion.6 = f32[8192,512]{1,0:T(8,128)} fusion(f32[8192,512]{1,0:T(8,128)} %constant_dynamic-update-slice_fusion.7, f32[1024,512]{1,0:T(8,128)} %collective-permute-done.1), kind=kLoop, calls=%fused_computation.9 | loop fusion | bytes 4194304
  159.8 3.1 %constant_dynamic-update-slice_fusion.5 = f32[8192,512]{1,0:T(8,128)} fusion(f32[8192,512]{1,0:T(8,128)} %constant_dynamic-update-slice_fusion.6, f32[1024,512]{1,0:T(8,128)} %copy-done.1), kind=kLoop, calls=%fused_computation.8 | loop fusion | bytes 4194304
  162.9 3.1 %constant_dynamic-update-slice_fusion.4 = f32[8192,512]{1,0:T(8,128)} fusion(f32[8192,512]{1,0:T(8,128)} %constant_dynamic-update-slice_fusion.5, f32[1024,512]{1,0:T(8,128)} %param.3), kind=kLoop, calls=%fused_computation.7 | loop fusion | bytes 4194304
  166.0 3.1 %constant_dynamic-update-slice_fusion.3 = f32[8192,512]{1,0:T(8,128)} fusion(f32[8192,512]{1,0:T(8,128)} %constant_dynamic-update-slice_fusion.4, f32[1024,512]{1,0:T(8,128)} %collective-permute-done.2), kind=kLoop, calls=%fused_computation.6 | loop fusion | bytes 4194304
  169.1 3.1 %constant_dynamic-update-slice_fusion.2 = f32[8192,512]{1,0:T(8,128)} fusion(f32[8192,512]{1,0:T(8,128)} %constant_dynamic-update-slice_fusion.3, f32[1024,512]{1,0:T(8,128)} %collective-permute-done.1), kind=kLoop, calls=%fused_computation.5 | loop fusion | bytes 4194304
  172.2 0.0 copy-done.2
  172.2 1.5 constant_dynamic-update-slice_fusion.1
  173.7 0.0 copy-done
  173.7 1.5 constant_dynamic-update-slice_fusion
  175.2 0.0 all-gather.2.cloned.1.call-done
  175.2 55.6 %fusion.2 = f32[1024,512]{0,1:T(8,128)S(1)} fusion(f32[1024,4096]{1,0:T(8,128)} %all-gather.2.cloned.1.call-done, f32[8192,512]{1,0:T(8,128)} %constant_dynamic-update-slice_fusion, s32[]{:T(128)S(6)} %select_n.14), kind=kOutput, calls=%fused_computation.2 | convolution fusion | flops 25769803776 | bytes 27262980 | tf_op jit(solution)/shard_map/dot_general | solution.py:8
  230.8 1.8 copy.3
Async XLA Ops:
  6.5 167.2 %copy-start = (f32[1024,512]{1,0:T(8,128)S(1)}, f32[1024,512]{1,0:T(8,128)}, u32[]{:S(2)}) copy-start(f32[1024,512]{1,0:T(8,128)} %param.3) | copy-start | bytes 6291460
  6.5 168.6 %all-gather.2.cloned.1.call-start = ((), (), s32[]{:S(2)}) async-start(), calls=%async_computation | async-start | bytes 18874368 | tf_op jit(solution)/shard_map/all_gather | solution.py:14
  7.3 49.8 %collective-permute-start = (f32[1024,512]{1,0:T(8,128)}, f32[1024,512]{1,0:T(8,128)S(1)}, u32[]{:S(2)}, u32[]{:S(2)}) collective-permute-start(f32[1024,512]{1,0:T(8,128)} %param.3), channel_id=1, source_target_pairs={{0,8},{8,16},{16,24},{24,0},{1,9},{9,17},{17,25},{25,1},{2,10},{10... | collective-permute-start | bytes 6291464 | tf_op jit(solution)/shard_map/ppermute | solution.py:17
  57.1 1.3 copy-start.1
  58.4 47.9 %collective-permute-start.1 = (f32[1024,512]{1,0:T(8,128)S(1)}, f32[1024,512]{1,0:T(8,128)}, u32[]{:S(2)}, u32[]{:S(2)}) collective-permute-start(f32[1024,512]{1,0:T(8,128)S(1)} %collective-permute-done), channel_id=1, source_target_pairs={{0,8},{8,16},{16,24},{24,0},{1,9},{9,17},{17,25},{25,1},{2,10},{10... | collective-permute-start | bytes 6291464 | tf_op jit(solution)/shard_map/ppermute | solution.py:17
  106.3 47.3 %collective-permute-start.2 = (f32[1024,512]{1,0:T(8,128)}, f32[1024,512]{1,0:T(8,128)}, u32[]{:S(2)}, u32[]{:S(2)}) collective-permute-start(f32[1024,512]{1,0:T(8,128)} %collective-permute-done.1), channel_id=1, source_target_pairs={{0,8},{8,16},{16,24},{24,0},{1,9},{9,17},{17,25},{25,1},{2,10},{10... | collective-permute-start | bytes 6291464 | tf_op jit(solution)/shard_map/ppermute | solution.py:17
  106.3 65.9 %copy-start.2 = (f32[1024,512]{1,0:T(8,128)S(1)}, f32[1024,512]{1,0:T(8,128)}, u32[]{:S(2)}) copy-start(f32[1024,512]{1,0:T(8,128)} %copy-done.1) | copy-start | bytes 6291460
Sparse Core Ops, SparseCore 0:
  8.9 153.7 all-gather.1
